TPU v7x, 32 devices: a whole 2x2x4 slice. The times are simulated.
32 devices in a mesh: img: 8 (over y, x, core), atom: 4 (over z).
Axes of the slice: x: 2, y: 2, z: 4, core: 2. Of those that a mesh axis runs over, the one named last changes fastest.
Arguments:
- positions: float32 [3, 256, 4096], P(None, 'img', 'atom'), may hold values from -6 to 6
- strength: float32 [4096], replicated, may hold values from 0.5 to 2
- tile_pairs: int32 [32, 8], replicated, may hold values from 0 to 31
- source_segment: int32 [256], P('img'), may hold values from 1 to 255, as said below
Outputs:
- string: float32 [3, 256, 4096], P(None, 'img', 'atom')
Inputs may be any that keep to these rules, and one draw needn't show every extreme that they name: source_segment[j] is j or j + 1, never 0 and never above 255.
All inputs are finite; a program needn't handle non-finite values.
Results may differ from a plain program's by a relative error of at most 0.0003.
Values sent between devices are 32-bit elements; how exact they have to be, the bound alone decides.
A program may use at most 64 MiB of HBM per device.

v0:
```python
import jax
import jax.numpy as jnp
from jax import lax
from jax.sharding import PartitionSpec as P

TB = 128


STEP_SIZE = 0.02


def padded(cells, sides, width):
    for axis, dim in sides:
        count = lax.axis_size(axis)
        ends = count - 1
        head = lax.slice_in_dim(cells, 0, width, axis=dim)
        tail = lax.slice_in_dim(cells, cells.shape[dim] - width, cells.shape[dim], axis=dim)
        cells = jnp.concatenate(
            [
                lax.ppermute(tail, axis, [(i, (i + 1) % count) for i in range(ends)]),
                cells,
                lax.ppermute(head, axis, [((i + 1) % count, i) for i in range(ends)]),
            ],
            axis=dim,
        )
    return cells


def pair_force(block_pos, block_strength, whole_pos, strength, partners):
    force_sum = jnp.zeros(block_pos.shape, jnp.float32)
    for neighbor_slot in range(partners.shape[0]):
        first_atom = partners[neighbor_slot] * TB
        partner_pos = lax.dynamic_slice_in_dim(whole_pos, first_atom, TB, 2)
        partner_strength = lax.dynamic_slice_in_dim(strength, first_atom, TB, 0)
        differ = block_pos[:, :, :, None] - partner_pos[:, :, None, :]
        radius = jnp.sum(differ * differ, axis=0)
        coupling = (
            block_strength[None, :, None] * partner_strength[None, None, :] * jnp.exp(-0.5 * radius)
        )
        force_sum = force_sum + jnp.sum(differ * coupling[None], axis=3)
    return force_sum


def block_forces(blocks, indices, strength, tile_pairs, whole_pos):

    def one_block(inputs):
        block_pos, index = inputs
        partners = tile_pairs[index]
        block_strength = lax.dynamic_slice_in_dim(strength, index * TB, TB, 0)
        return pair_force(block_pos, block_strength, whole_pos, strength, partners)

    result = lax.map(one_block, (blocks, indices))
    block_count, _, image_count, _ = result.shape
    return result.transpose(1, 2, 0, 3).reshape(3, image_count, block_count * TB)


def shards(positions, strength, tile_pairs, source_segment):
    count = positions.shape[1]
    local_atoms = positions.shape[2]
    whole_pos = lax.all_gather(positions, "atom", axis=2, tiled=True)
    per_device = local_atoms // TB
    blocks = positions.reshape(3, count, per_device, TB).transpose(2, 0, 1, 3)
    indices = lax.axis_index("atom") * per_device + jnp.arange(per_device, dtype=jnp.int32)
    forces = block_forces(blocks, indices, strength, tile_pairs, whole_pos)
    moved = positions + STEP_SIZE * forces
    first_image = lax.axis_index("img") * count
    images_total = count * lax.axis_size("img")
    extended = padded(moved, (("img", 1),), 1)
    segments = extended[:, 1:] - extended[:, :-1]
    partial_value = jnp.sum(segments * segments, axis=(0, 2))
    squares = lax.psum(partial_value, "atom")
    global_ids = first_image + jnp.arange(count + 1, dtype=jnp.int32)
    valid = (global_ids >= 1) & (global_ids <= images_total - 1)
    lengths = jnp.where(valid, jnp.sqrt(1.0 + squares), jnp.zeros_like(squares))
    running = jnp.cumsum(lengths[:count])
    device_total = running[-1]
    totals = lax.all_gather(device_total[None], "img", axis=0, tiled=True)
    ranks = jnp.arange(totals.shape[0], dtype=jnp.int32)
    offset = jnp.sum(jnp.where(ranks < lax.axis_index("img"), totals, jnp.zeros_like(totals)))
    total_arc = jnp.sum(totals)
    arc_ext = jnp.concatenate(
        [offset[None], offset + running, (offset + device_total + lengths[count])[None]]
    )
    length_ext = jnp.concatenate([jnp.zeros((1,), jnp.float32), lengths])
    upper = source_segment - first_image + 1
    lower = upper - 1
    columns = jnp.arange(count + 2, dtype=jnp.int32)
    hit_low = (columns[None, :] == lower[:, None]).astype(jnp.float32)
    hit_high = (columns[None, :] == upper[:, None]).astype(jnp.float32)
    arc_low = jnp.sum(hit_low * arc_ext[None, :], axis=1)
    seg_length = jnp.sum(hit_high * length_ext[None, :], axis=1)
    target = (first_image + jnp.arange(count, dtype=jnp.int32)).astype(jnp.float32) * (
        total_arc / (images_total - 1)
    )
    weight = (target - arc_low) / seg_length
    mixing = (1.0 - weight)[:, None] * hit_low + weight[:, None] * hit_high
    string = jnp.einsum("je,cea->cja", mixing, extended, precision=lax.Precision.HIGHEST)
    return string


def solution(mesh):
    placed = (P(None, "img", "atom"), P(), P(), P("img"))
    return jax.shard_map(
        shards, mesh=mesh, in_specs=placed, out_specs=P(None, "img", "atom"), check_vma=False
    )
```

profile of v0, /device:TPU:4, one launch (start us, length us, event | category | flops | bytes accessed | tf_op | source)
XLA Modules:
  0.0 445.6 jit_solution(13500189040580754193)
XLA Ops:
  7.3 1.1 copy.15
  8.4 38.8 %all-gather.3.cloned.1.call-done = f32[3,32,4096]{2,1,0:T(8,128)} async-done(((f32[3,32,1024]{2,1,0:T(8,128)}), f32[3,32,4096]{2,1,0:T(8,128)}) %all-gather.3.cloned.1.call-update) | async-done | bytes 1572880 | tf_op jit(solution)/shard_map/all_gather | solution.py:60
  47.2 351.6 %while.10 = (s32[]{:T(128)}, f32[8,3,32,128]{3,2,1,0:T(8,128)}, f32[8,3,32,128]{3,0,2,1:T(8,128)S(1)}, s32[8]{0:T(128)S(1)}, s32[32,8]{0,1:T(8,128)}, /*index=5*...) while((s32[]{:T(128)}, f32[8,3,32,128]{3,2,1,0:T(8,128)}, ...), condition=%wide.region_17.18_spmd, body=%wide.region_0.17_spmd.sunk | while | flops 79810600 | bytes 70826768 | solution.py:52
  49.4 0.8 constant_dynamic-slice_fusion.13
  55.8 1.0 constant_dynamic-slice_fusion.14
  56.9 3.7 fusion.45
  61.2 0.9 fusion.46
  62.2 2.1 exponential_multiply_fusion.15
  64.4 10.2 %fusion.47 = (f32[3,32,128]{2,1,0:T(8,128)S(1)}, f32[32,128,128]{2,1,0:T(8,128)S(1)}, f32[32,128,128]{2,1,0:T(8,128)S(1)}, f32[32,128,128]{2,1,0:T(8,128)S(1)}, ...) fusion(f32[32,128,128]{2,1,0:T(8,128)S(1)} %get-tuple-element.2, ...), kind=kLoop, calls=%fused_computation.19.clone.1 | loop fusion | flops 34578432 | bytes 17317888 | tf_op jit(solution)/shard_map/while/body/eval_jaxpr/reduce_sum | solution.py:40
  76.3 14.1 %fusion.48 = (f32[3,32,128]{2,1,0:T(8,128)S(1)}, f32[3,32,128]{2,1,0:T(8,128)S(1)}, f32[3,32,128]{2,1,0:T(8,128)S(1)}, f32[3,32,128]{2,1,0:T(8,128)S(1)}, f32[3,...) fusion(f32[32,128,128]{2,1,0:T(8,128)S(1)} %exponential_multiply_fusion.16, ...), kind=kLoop, calls=%fused_computation.21.clone.1 | loop fusion | flops 28237824 | bytes 13221888 | tf_op jit(solution)/shard_map/while/body/eval_jaxpr/reduce_sum | solution.py:40
  99.8 1.0 constant_dynamic-slice_fusion.14
  100.8 3.7 fusion.45
  105.1 0.9 fusion.46
  106.1 2.1 exponential_multiply_fusion.15
  108.3 10.2 %fusion.47 = (f32[3,32,128]{2,1,0:T(8,128)S(1)}, f32[32,128,128]{2,1,0:T(8,128)S(1)}, f32[32,128,128]{2,1,0:T(8,128)S(1)}, f32[32,128,128]{2,1,0:T(8,128)S(1)}, ...) fusion(f32[32,128,128]{2,1,0:T(8,128)S(1)} %get-tuple-element.2, ...), kind=kLoop, calls=%fused_computation.19.clone.1 | loop fusion | flops 34578432 | bytes 17317888 | tf_op jit(solution)/shard_map/while/body/eval_jaxpr/reduce_sum | solution.py:40
  120.2 14.1 %fusion.48 = (f32[3,32,128]{2,1,0:T(8,128)S(1)}, f32[3,32,128]{2,1,0:T(8,128)S(1)}, f32[3,32,128]{2,1,0:T(8,128)S(1)}, f32[3,32,128]{2,1,0:T(8,128)S(1)}, f32[3,...) fusion(f32[32,128,128]{2,1,0:T(8,128)S(1)} %exponential_multiply_fusion.16, ...), kind=kLoop, calls=%fused_computation.21.clone.1 | loop fusion | flops 28237824 | bytes 13221888 | tf_op jit(solution)/shard_map/while/body/eval_jaxpr/reduce_sum | solution.py:40
  137.3 0.8 constant_dynamic-slice_fusion.13
  143.7 1.0 constant_dynamic-slice_fusion.14
  144.8 3.7 fusion.45
  149.0 1.0 fusion.46
  150.1 2.1 exponential_multiply_fusion.15
  152.3 10.2 %fusion.47 = (f32[3,32,128]{2,1,0:T(8,128)S(1)}, f32[32,128,128]{2,1,0:T(8,128)S(1)}, f32[32,128,128]{2,1,0:T(8,128)S(1)}, f32[32,128,128]{2,1,0:T(8,128)S(1)}, ...) fusion(f32[32,128,128]{2,1,0:T(8,128)S(1)} %get-tuple-element.2, ...), kind=kLoop, calls=%fused_computation.19.clone.1 | loop fusion | flops 34578432 | bytes 17317888 | tf_op jit(solution)/shard_map/while/body/eval_jaxpr/reduce_sum | solution.py:40
  164.2 14.1 %fusion.48 = (f32[3,32,128]{2,1,0:T(8,128)S(1)}, f32[3,32,128]{2,1,0:T(8,128)S(1)}, f32[3,32,128]{2,1,0:T(8,128)S(1)}, f32[3,32,128]{2,1,0:T(8,128)S(1)}, f32[3,...) fusion(f32[32,128,128]{2,1,0:T(8,128)S(1)} %exponential_multiply_fusion.16, ...), kind=kLoop, calls=%fused_computation.21.clone.1 | loop fusion | flops 28237824 | bytes 13221888 | tf_op jit(solution)/shard_map/while/body/eval_jaxpr/reduce_sum | solution.py:40
  181.3 0.8 constant_dynamic-slice_fusion.13
  187.7 1.0 constant_dynamic-slice_fusion.14
  188.8 3.7 fusion.45
  193.0 1.0 fusion.46
  194.1 2.1 exponential_multiply_fusion.15
  196.2 10.2 %fusion.47 = (f32[3,32,128]{2,1,0:T(8,128)S(1)}, f32[32,128,128]{2,1,0:T(8,128)S(1)}, f32[32,128,128]{2,1,0:T(8,128)S(1)}, f32[32,128,128]{2,1,0:T(8,128)S(1)}, ...) fusion(f32[32,128,128]{2,1,0:T(8,128)S(1)} %get-tuple-element.2, ...), kind=kLoop, calls=%fused_computation.19.clone.1 | loop fusion | flops 34578432 | bytes 17317888 | tf_op jit(solution)/shard_map/while/body/eval_jaxpr/reduce_sum | solution.py:40
  208.1 14.1 %fusion.48 = (f32[3,32,128]{2,1,0:T(8,128)S(1)}, f32[3,32,128]{2,1,0:T(8,128)S(1)}, f32[3,32,128]{2,1,0:T(8,128)S(1)}, f32[3,32,128]{2,1,0:T(8,128)S(1)}, f32[3,...) fusion(f32[32,128,128]{2,1,0:T(8,128)S(1)} %exponential_multiply_fusion.16, ...), kind=kLoop, calls=%fused_computation.21.clone.1 | loop fusion | flops 28237824 | bytes 13221888 | tf_op jit(solution)/shard_map/while/body/eval_jaxpr/reduce_sum | solution.py:40
  225.2 0.8 constant_dynamic-slice_fusion.13
  231.6 1.0 constant_dynamic-slice_fusion.14
  232.7 3.7 fusion.45
  236.9 0.9 fusion.46
  238.0 2.1 exponential_multiply_fusion.15
  240.2 10.2 %fusion.47 = (f32[3,32,128]{2,1,0:T(8,128)S(1)}, f32[32,128,128]{2,1,0:T(8,128)S(1)}, f32[32,128,128]{2,1,0:T(8,128)S(1)}, f32[32,128,128]{2,1,0:T(8,128)S(1)}, ...) fusion(f32[32,128,128]{2,1,0:T(8,128)S(1)} %get-tuple-element.2, ...), kind=kLoop, calls=%fused_computation.19.clone.1 | loop fusion | flops 34578432 | bytes 17317888 | tf_op jit(solution)/shard_map/while/body/eval_jaxpr/reduce_sum | solution.py:40
  252.1 14.1 %fusion.48 = (f32[3,32,128]{2,1,0:T(8,128)S(1)}, f32[3,32,128]{2,1,0:T(8,128)S(1)}, f32[3,32,128]{2,1,0:T(8,128)S(1)}, f32[3,32,128]{2,1,0:T(8,128)S(1)}, f32[3,...) fusion(f32[32,128,128]{2,1,0:T(8,128)S(1)} %exponential_multiply_fusion.16, ...), kind=kLoop, calls=%fused_computation.21.clone.1 | loop fusion | flops 28237824 | bytes 13221888 | tf_op jit(solution)/shard_map/while/body/eval_jaxpr/reduce_sum | solution.py:40
  275.6 1.0 constant_dynamic-slice_fusion.14
  276.6 3.7 fusion.45
  280.9 1.0 fusion.46
  282.0 2.1 exponential_multiply_fusion.15
  284.1 10.2 %fusion.47 = (f32[3,32,128]{2,1,0:T(8,128)S(1)}, f32[32,128,128]{2,1,0:T(8,128)S(1)}, f32[32,128,128]{2,1,0:T(8,128)S(1)}, f32[32,128,128]{2,1,0:T(8,128)S(1)}, ...) fusion(f32[32,128,128]{2,1,0:T(8,128)S(1)} %get-tuple-element.2, ...), kind=kLoop, calls=%fused_computation.19.clone.1 | loop fusion | flops 34578432 | bytes 17317888 | tf_op jit(solution)/shard_map/while/body/eval_jaxpr/reduce_sum | solution.py:40
  296.0 14.1 %fusion.48 = (f32[3,32,128]{2,1,0:T(8,128)S(1)}, f32[3,32,128]{2,1,0:T(8,128)S(1)}, f32[3,32,128]{2,1,0:T(8,128)S(1)}, f32[3,32,128]{2,1,0:T(8,128)S(1)}, f32[3,...) fusion(f32[32,128,128]{2,1,0:T(8,128)S(1)} %exponential_multiply_fusion.16, ...), kind=kLoop, calls=%fused_computation.21.clone.1 | loop fusion | flops 28237824 | bytes 13221888 | tf_op jit(solution)/shard_map/while/body/eval_jaxpr/reduce_sum | solution.py:40
  319.5 1.0 constant_dynamic-slice_fusion.14
  320.6 3.7 fusion.45
  324.8 0.9 fusion.46
  325.9 2.1 exponential_multiply_fusion.15
  328.0 10.2 %fusion.47 = (f32[3,32,128]{2,1,0:T(8,128)S(1)}, f32[32,128,128]{2,1,0:T(8,128)S(1)}, f32[32,128,128]{2,1,0:T(8,128)S(1)}, f32[32,128,128]{2,1,0:T(8,128)S(1)}, ...) fusion(f32[32,128,128]{2,1,0:T(8,128)S(1)} %get-tuple-element.2, ...), kind=kLoop, calls=%fused_computation.19.clone.1 | loop fusion | flops 34578432 | bytes 17317888 | tf_op jit(solution)/shard_map/while/body/eval_jaxpr/reduce_sum | solution.py:40
  339.9 14.1 %fusion.48 = (f32[3,32,128]{2,1,0:T(8,128)S(1)}, f32[3,32,128]{2,1,0:T(8,128)S(1)}, f32[3,32,128]{2,1,0:T(8,128)S(1)}, f32[3,32,128]{2,1,0:T(8,128)S(1)}, f32[3,...) fusion(f32[32,128,128]{2,1,0:T(8,128)S(1)} %exponential_multiply_fusion.16, ...), kind=kLoop, calls=%fused_computation.21.clone.1 | loop fusion | flops 28237824 | bytes 13221888 | tf_op jit(solution)/shard_map/while/body/eval_jaxpr/reduce_sum | solution.py:40
  363.4 1.1 constant_dynamic-slice_fusion.14
  364.6 3.7 fusion.45
  368.8 0.9 fusion.46
  369.9 2.1 exponential_multiply_fusion.15
  372.0 10.2 %fusion.47 = (f32[3,32,128]{2,1,0:T(8,128)S(1)}, f32[32,128,128]{2,1,0:T(8,128)S(1)}, f32[32,128,128]{2,1,0:T(8,128)S(1)}, f32[32,128,128]{2,1,0:T(8,128)S(1)}, ...) fusion(f32[32,128,128]{2,1,0:T(8,128)S(1)} %get-tuple-element.2, ...), kind=kLoop, calls=%fused_computation.19.clone.1 | loop fusion | flops 34578432 | bytes 17317888 | tf_op jit(solution)/shard_map/while/body/eval_jaxpr/reduce_sum | solution.py:40
  383.9 14.1 %fusion.48 = (f32[3,32,128]{2,1,0:T(8,128)S(1)}, f32[3,32,128]{2,1,0:T(8,128)S(1)}, f32[3,32,128]{2,1,0:T(8,128)S(1)}, f32[3,32,128]{2,1,0:T(8,128)S(1)}, f32[3,...) fusion(f32[32,128,128]{2,1,0:T(8,128)S(1)} %exponential_multiply_fusion.16, ...), kind=kLoop, calls=%fused_computation.21.clone.1 | loop fusion | flops 28237824 | bytes 13221888 | tf_op jit(solution)/shard_map/while/body/eval_jaxpr/reduce_sum | solution.py:40
  398.7 1.0 bitcast_add_fusion
  399.8 1.9 collective-permute-start
  401.7 4.5 %collective-permute-start.1 = (f32[3,1,1024]{2,1,0:T(1,128)S(1)}, f32[3,1,1024]{2,1,0:T(1,128)S(1)}, u32[]{:S(2)}, u32[]{:S(2)}) collective-permute-start(f32[3,1,1024]{2,1,0:T(1,128)S(1)} %get-tuple-element.129), channel_id=1, source_target_pairs={{4,0},{8,4},{12,8},{16,12},{20,16},{24,20},{28,24},{5,1},{9,5},{13... | collective-permute-start | bytes 36872 | tf_op jit(solution)/shard_map/ppermute | solution.py:22
  407.9 9.5 %psum.7 = f32[33]{0:T(128)S(1)} all-reduce(f32[33]{0:T(128)S(1)} %fusion.22), channel_id=1, replica_groups=mesh['img'=8,'atom'=4] {'atom'}, use_global_device_ids=true, to_apply=%region_19.20 | all-reduce | flops 33 | bytes 264 | tf_op jit(solution)/shard_map/psum | solution.py:71
  418.1 1.3 bitcast_dynamic-update-slice_fusion.1
  420.0 12.4 %all-reduce = f32[8]{0:T(128)S(1)} all-reduce(f32[8]{0:T(128)S(1)} %bitcast_dynamic-update-slice_fusion.1), channel_id=2, replica_groups=mesh['img'=8,'atom'=4] {'img'}, use_global_device_ids=true, to_apply=%add | all-reduce | flops 8 | bytes 64 | tf_op jit(solution)/shard_map/all_gather | solution.py:77
  433.0 0.8 add_reduce_fusion
  436.4 0.8 pad_maximum_fusion
  437.4 1.3 convolution_bitcast_fusion
  (120 shorter events, 37.3 us)
Async XLA Ops:
  6.5 40.6 %all-gather.3.cloned.1.call-start = ((), (), s32[]{:S(2)}) async-start(), calls=%async_computation | async-start | bytes 1966080 | tf_op jit(solution)/shard_map/all_gather | solution.py:60
  47.2 351.6 %copy-start = (f32[3,32,1024]{2,1,0:T(8,128)S(1)}, f32[3,32,1024]{2,1,0:T(8,128)}, u32[]{:S(2)}) copy-start(f32[3,32,1024]{2,1,0:T(8,128)} %param.6) | copy-start | bytes 1179652
  47.2 359.1 %copy-start.1 = (s32[32]{0:T(128)S(1)}, s32[32]{0:T(128)}, u32[]{:S(2)}) copy-start(s32[32]{0:T(128)} %param.9) | copy-start | bytes 388
  47.2 359.1 %copy-start.2 = (u32[32]{0:T(128)S(1)}, u32[32]{0:T(128)}, u32[]{:S(2)}) copy-start(u32[32]{0:T(128)} %constant.75) | copy-start | bytes 388
  399.8 7.1 %collective-permute-start = (f32[3,1,1024]{2,1,0:T(1,128)S(1)}, f32[3,1,1024]{2,1,0:T(1,128)S(1)}, u32[]{:S(2)}, u32[]{:S(2)}) collective-permute-start(f32[3,1,1024]{2,1,0:T(1,128)S(1)} %get-tuple-element.128), channel_id=1, source_target_pairs={{0,4},{4,8},{8,12},{12,16},{16,20},{20,24},{24,28},{1,5},{5,9},{9,... | collective-permute-start | bytes 36872 | tf_op jit(solution)/shard_map/ppermute | solution.py:20
  401.7 5.9 %collective-permute-start.1 = (f32[3,1,1024]{2,1,0:T(1,128)S(1)}, f32[3,1,1024]{2,1,0:T(1,128)S(1)}, u32[]{:S(2)}, u32[]{:S(2)}) collective-permute-start(f32[3,1,1024]{2,1,0:T(1,128)S(1)} %get-tuple-element.129), channel_id=1, source_target_pairs={{4,0},{8,4},{12,8},{16,12},{20,16},{24,20},{28,24},{5,1},{9,5},{13... | collective-permute-start | bytes 36872 | tf_op jit(solution)/shard_map/ppermute | solution.py:22
Sparse Core Ops, SparseCore 0:
  8.9 38.2 all-gather.2
where the time goes:
time: 448 us; the launch traced here: 446 us
  other arithmetic  264 us (59%)
  loops' own time  58.9 us (13%)
  waiting for transfers between devices  40.2 us (9%)
  local copies, waits for them, and re-layouts  36.3 us (8%)
  blocking collectives  21.9 us (5%)
  between operations  16.1 us (4%)
  starting transfers between devices  6.46 us (1%)
    reduce_sum x16, other arithmetic, pair_force(): force_sum = force_sum + jnp.sum(differ * coupling[None], axis=3)  194 us
    another operation x1, loops' own time, block_forces(): result = lax.map(one_block, (blocks, indices))  58.9 us
    all_gather x1, waiting for transfers between devices, shards(): whole_pos = lax.all_gather(positions, 'atom', axis=2, tiled=True)  38.8 us
    mul x64, other arithmetic, pair_force(): block_strength[None, :, None] * partner_strength[None, None, :]  31.5 us
    reduce_sum x8, other arithmetic, pair_force(): radius = jnp.sum(differ * differ, axis=0)  29.4 us
    all_gather x1, blocking collectives, shards(): totals = lax.all_gather(device_total[None], 'img', axis=0, tiled=True)  12.4 us
    psum x1, blocking collectives, shards(): squares = lax.psum(partial_value, 'atom')  9.51 us
  transfers between devices with their start and end apart: 3, of which 2 were waited for; matrix products, arithmetic and copies ran while one was open for 0% of the time, Pallas kernels for 0%

commit v1 on v0

v1 whole, which is shorter than its diff:
```python
import functools
import math

import jax
import jax.numpy as jnp
from jax import lax
from jax.experimental import pallas as pl
from jax.experimental.pallas import tpu as pltpu
from jax.sharding import PartitionSpec as P

TB = 128
STEP_SIZE = 0.02
LOG2E = math.log2(math.e)
F32 = jnp.float32
BF16 = jnp.bfloat16


def split3(v):
    h = v.astype(BF16).astype(F32)
    r = v - h
    m = r.astype(BF16).astype(F32)
    return h, m, r - m


def features(x0, x1, x2, logs):
    shape = (8, x0.shape[1])
    row = lax.broadcasted_iota(jnp.int32, shape, 0)
    comp = row & 3
    low = row < 4
    half = (-0.5 * LOG2E) * (x0 * x0 + x1 * x1 + x2 * x2)
    x0, x1, x2 = (jnp.broadcast_to(v, shape) for v in (x0, x1, x2))
    norm_j = jnp.broadcast_to(half + logs, shape)
    norm_i = jnp.broadcast_to(half, shape)
    xs = jnp.where(comp == 0, x0, jnp.where(comp == 1, x1, x2))
    h, m, l = split3(jnp.where(comp == 3, norm_j, xs))
    ones = jnp.where(row < 3, 1.0, 0.0).astype(F32)
    key = jnp.concatenate([h, jnp.where(low, h, m), jnp.where(low, m, l), ones], axis=0)
    bh, bm, bl = split3(jnp.where(comp == 3, 1.0, LOG2E * xs))
    ph, pm, plo = split3(norm_i)
    tail = jnp.where(row == 0, ph, jnp.where(row == 1, pm, jnp.where(row == 2, plo, 0.0)))
    query = jnp.concatenate(
        [jnp.where(low, bh, bm), jnp.where(low, bl, bh), jnp.where(low, bm, bh), tail], axis=0
    )
    v0 = jnp.where(comp == 3, jnp.where(low, 1.0, 0.0), jnp.where(low, h, m))
    v1 = jnp.where(row < 3, l, 0.0)
    value = jnp.concatenate([v0, v1], axis=0)
    return query, key, value


def force_kernel(x_ref, s_ref, pairs_ref, out_ref, query_ref, key_ref, value_ref):
    images = x_ref.shape[1]
    tiles = x_ref.shape[2] // TB
    neighbors = pairs_ref.shape[1]

    for pair in range(images // 2):

        @pl.loop(0, tiles)
        def _(t, pair=pair):
            lanes = pl.ds(pl.multiple_of(t * TB, TB), TB)
            logs = jnp.log2(s_ref[:, lanes])
            (qa, ka, va), (qb, kb, vb) = (
                features(*(x_ref[c, pl.ds(image, 1), lanes] for c in range(3)), logs)
                for image in (2 * pair, 2 * pair + 1)
            )
            zero = jnp.zeros_like(qa)
            query_ref[pair, t] = jnp.concatenate(
                [jnp.concatenate([qa, zero], axis=1), jnp.concatenate([zero, qb], axis=1)], axis=0
            ).astype(BF16)
            keys = jnp.concatenate([ka, kb, jnp.zeros_like(ka), jnp.zeros_like(kb)], axis=0)
            key_ref[pair, t] = keys.T.astype(BF16)
            values = jnp.concatenate([va, vb], axis=0).astype(BF16)
            value_ref[pair, t] = jnp.concatenate([values, values], axis=1)

    for pair in range(images // 2):

        @pl.loop(0, tiles)
        def _(b, pair=pair):
            query = query_ref[pair, b]
            total = jnp.zeros((32, 2 * TB), F32)
            for slot in range(neighbors):
                t = pairs_ref[b, slot]
                power = jnp.dot(key_ref[pair, t][:, :64], query, preferred_element_type=F32)
                weight = jnp.exp2(power)
                hi = weight.astype(BF16)
                lo = (weight - hi.astype(F32)).astype(BF16)
                total = total + jnp.dot(
                    value_ref[pair, t],
                    jnp.concatenate([hi, lo], axis=0),
                    preferred_element_type=F32,
                )
            lanes = pl.ds(pl.multiple_of(b * TB, TB), TB)
            step = STEP_SIZE * s_ref[:, lanes]
            for side in range(2):
                block = total[16 * side : 16 * side + 16, side * TB : (side + 1) * TB]
                weight_sum = block[3:4]
                for c in range(3):
                    moment = block[c : c + 1] + block[4 + c : 5 + c] + block[8 + c : 9 + c]
                    x = x_ref[c, pl.ds(2 * pair + side, 1), lanes]
                    out_ref[c, pl.ds(2 * pair + side, 1), lanes] = x + step * (
                        x * weight_sum - moment
                    )


def moved_images(x, strength, tile_pairs):
    _, images, atoms = x.shape
    tiles = atoms // TB
    pairs = images // 2
    vmem = pl.BlockSpec(memory_space=pltpu.VMEM)
    return pl.pallas_call(
        force_kernel,
        out_shape=jax.ShapeDtypeStruct(x.shape, F32),
        in_specs=[vmem, vmem, pl.BlockSpec(memory_space=pltpu.SMEM)],
        out_specs=vmem,
        scratch_shapes=[
            pltpu.VMEM((pairs, tiles, 64, 2 * TB), BF16),
            pltpu.VMEM((pairs, tiles, TB, TB), BF16),
            pltpu.VMEM((pairs, tiles, 32, 2 * TB), BF16),
        ],
        compiler_params=pltpu.CompilerParams(vmem_limit_bytes=48 * 1024 * 1024),
    )(x, strength.reshape(1, atoms), tile_pairs)


def shards(positions, strength, tile_pairs, source_segment):
    atom_devices = lax.axis_size("atom")
    img_devices = lax.axis_size("img")
    ring = img_devices * atom_devices
    x = lax.all_to_all(positions, "atom", split_axis=1, concat_axis=2, tiled=True)
    images = x.shape[1]
    images_total = images * ring
    moved = moved_images(x, strength, tile_pairs)
    axes = ("img", "atom")
    before = lax.ppermute(moved[:, -1:], axes, [(i, i + 1) for i in range(ring - 1)])
    after = lax.ppermute(moved[:, :1], axes, [(i + 1, i) for i in range(ring - 1)])
    extended = jnp.concatenate([before, moved, after], axis=1)
    segments = extended[:, 1:-1] - extended[:, :-2]
    squares = jnp.sum(segments * segments, axis=(0, 2))
    everyone = lax.all_gather(squares, axes, axis=0, tiled=True)
    ids = jnp.arange(images_total, dtype=jnp.int32)
    lengths = jnp.where(ids >= 1, jnp.sqrt(1.0 + everyone), 0.0)
    first = (lax.axis_index("img") * atom_devices + lax.axis_index("atom")) * images
    mine = lax.dynamic_slice_in_dim(
        source_segment, lax.axis_index("atom") * images, images, 0
    )
    total_arc = jnp.sum(lengths)
    arc_low = jnp.sum(jnp.where(ids[None, :] < mine[:, None], lengths[None, :], 0.0), axis=1)
    seg_length = jnp.sum(jnp.where(ids[None, :] == mine[:, None], lengths[None, :], 0.0), axis=1)
    own = first + jnp.arange(images, dtype=jnp.int32)
    target = own.astype(F32) * (total_arc / (images_total - 1))
    weight = ((target - arc_low) / seg_length)[None, :, None]
    later = (mine > own)[None, :, None]
    low = jnp.where(later, extended[:, 1:-1], extended[:, :-2])
    high = jnp.where(later, extended[:, 2:], extended[:, 1:-1])
    string = (1.0 - weight) * low + weight * high
    return lax.all_to_all(string, "atom", split_axis=2, concat_axis=1, tiled=True)


def solution(mesh):
    placed = (P(None, "img", "atom"), P(), P(), P("img"))
    return jax.shard_map(
        shards, mesh=mesh, in_specs=placed, out_specs=P(None, "img", "atom"), check_vma=False
    )
```

time: 448 us -> 222 us (0.50)
  other arithmetic: 264 us -> 3.72 us
  Pallas kernels: 0 us -> 103 us
  loops' own time: 58.9 us -> 0 us
  blocking collectives: 21.9 us -> 52.5 us
  waiting for transfers between devices: 40.2 us -> 13.7 us
  between operations: 16.1 us -> 0.74 us
  starting transfers between devices: 6.46 us -> 14 us
    reduce_sum x27 -> x3, other arithmetic: 225 us -> 1.01 us  [the longest x1 0.61 us: shards(): total_arc = jnp.sum(lengths)]
    pallas_call x0 -> x1, Pallas kernels: none -> 103 us  [moved_images(): pl.pallas_call(force_kernel, out_shape=jax.ShapeDtypeStruct(x.shape, F32)...]
    another operation x1 -> x0, loops' own time: 58.9 us -> none  [block_forces(): result = lax.map(one_block, (blocks, indices))]
    all_gather x1 -> x0, waiting for transfers between devices: 38.8 us -> none  [shards(): whole_pos = lax.all_gather(positions, 'atom', axis=2, tiled=True)]
    unnamed x0 -> x1, blocking collectives: none -> 37.6 us
    mul x64 -> x0, other arithmetic: 31.5 us -> none  [pair_force(): block_strength[None, :, None] * partner_strength[None, None, :]]
    dynamic_slice x40 -> x0, local copies, waits for them, and re-layouts: 27 us -> none  [the longest x8 8.21 us: pair_force(): partner_pos = lax.dynamic_slice_in_dim(whole_pos, first_atom, TB, 2)]
    unnamed x10 -> x8, local copies, waits for them, and re-layouts: 2.97 us -> 19.3 us
  transfers between devices with their start and end apart: 3 -> 3, of which waited for: 2 -> 1; matrix products, arithmetic and copies ran while one was open for 0% -> 1% of each run, Pallas kernels for 0% -> 0%
where the time goes in v1:
time: 222 us; the launch traced here: 221 us
  Pallas kernels  103 us (46%)
  blocking collectives  52.5 us (24%)
  local copies, waits for them, and re-layouts  33.3 us (15%)
  starting transfers between devices  14 us (6%)
  waiting for transfers between devices  13.7 us (6%)
  other arithmetic  3.72 us (2%)
    pallas_call x1, Pallas kernels, moved_images(): pl.pallas_call(force_kernel, out_shape=jax.ShapeDtypeStruct(x.shape, F32)...  103 us
    unnamed x1, blocking collectives  37.6 us
    unnamed x8, local copies, waits for them, and re-layouts  19.3 us
    all_to_all x1, blocking collectives, shards(): lax.all_to_all(string, 'atom', split_axis=2, concat_axis=1, tiled=True)  14.9 us
    all_to_all x1, waiting for transfers between devices, shards(): lax.all_to_all(positions, 'atom', split_axis=1, concat_axis=2, tiled=True)  13.7 us
    all_to_all x2, local copies, waits for them, and re-layouts, shards(): lax.all_to_all(string, 'atom', split_axis=2, concat_axis=1, tiled=True)  7.87 us
    ppermute x1, starting transfers between devices, shards(): lax.ppermute(moved[:, :1], axes, [(i + 1, i) for i in range(ring - 1)])  7.23 us
    add x1, local copies, waits for them, and re-layouts, shards(): string = (1.0 - weight) * low + weight * high  5.87 us
  transfers between devices with their start and end apart: 3, of which 1 were waited for; matrix products, arithmetic and copies ran while one was open for 1% of the time, Pallas kernels for 0%

profile of v1, /device:TPU:4, one launch (start us, length us, event | category | flops | bytes accessed | tf_op | source)
XLA Modules:
  0.0 221.0 jit_solution(7239161234867306906)
XLA Ops:
  0.0 2.1 copy.11
  2.1 4.9 %all-to-all-start = ((f32[3,32,1024]{2,0,1:T(4,128)}), f32[3,32,1024]{2,0,1:T(4,128)S(1)}, u32[]{:S(2)}, u32[]{:S(2)}) async-start(f32[3,32,1024]{2,0,1:T(4,128)} %copy.11), calls=%async_computation | async-start | bytes 1048576 | tf_op jit(solution)/shard_map/all_to_all | solution.py:127
  6.9 0.8 copy.13.pairs_ref
  7.7 13.7 %all-to-all-done = f32[3,32,1024]{2,0,1:T(4,128)S(1)} async-done(((f32[3,32,1024]{2,0,1:T(4,128)}), f32[3,32,1024]{2,0,1:T(4,128)S(1)}, u32[]{:S(2)}, u32[]{:S(2)}) %all-to-all-start) | async-done | bytes 393248 | tf_op jit(solution)/shard_map/all_to_all | solution.py:127
  21.4 0.2 copy.12
  21.7 0.0 copy-start
  21.7 0.7 copy-done
  22.4 102.9 %shard_map.46 = f32[3,8,4096]{2,1,0:T(8,128)S(1)} custom-call(f32[3,8,4096]{2,1,0:T(8,128)S(1)} %bitcast.11, f32[1,4096]{1,0:T(1,128)S(1)} %bitcast.12, s32[32,8]{1,0:T(8,128)S(1)} %copy.13.pairs_ref), custom_call_target="tpu_custom_call" | custom-call | tf_op jit(solution)/shard_map/pallas_call | solution.py:109
  125.3 0.1 fusion.10
  125.4 1.9 collective-permute-start
  127.3 0.7 fusion.8
  128.0 7.2 %collective-permute-start.1 = (f32[3,1,4096]{2,1,0:T(1,128)S(1)}, f32[3,1,4096]{2,1,0:T(1,128)S(1)}, u32[]{:S(2)}, u32[]{:S(2)}) collective-permute-start(f32[3,1,4096]{2,1,0:T(1,128)S(1)} %get-tuple-element.12), channel_id=1, source_target_pairs={{1,0},{2,1},{3,2},{4,3},{5,4},{6,5},{7,6},{8,7},{9,8},{10,9},{11,1... | collective-permute-start | bytes 147464 | tf_op jit(solution)/shard_map/ppermute | solution.py:133
  135.3 0.0 collective-permute-done
  135.3 0.2 fusion.7
  135.5 0.2 dynamic-update-slice
  135.7 37.6 %all-reduce = f32[256]{0:T(256)S(1)} all-reduce(f32[256]{0:T(256)S(1)} %dynamic-update-slice), channel_id=1, replica_groups=mesh['img'=8,'atom'=4] {'img','atom'}, use_global_device_ids=true, to_apply=%add | all-reduce | flops 256 | bytes 2048
  173.4 0.6 fusion.9
  174.0 0.2 select_reduce_fusion.1
  174.8 0.0 collective-permute-done.1
  174.8 0.2 fusion.2
  175.1 5.9 %copy.14 = f32[3,8,4096]{1,0,2:T(4,128)} copy(f32[3,8,4096]{2,1,0:T(8,128)S(1)} %fusion.2) | data formatting | bytes 786432 | tf_op jit(solution)/shard_map/add | solution.py:153
  180.9 6.9 %reshape.29 = f32[4,1,24576]{2,1,0:T(1,128)S(1)} reshape(f32[4096,3,8]{2,1,0:T(4,128)} %bitcast.13) | data formatting | bytes 786432
  187.8 14.9 %all_to_all.36 = f32[4,1,24576]{2,1,0:T(1,128)S(1)} all-to-all(f32[4,1,24576]{2,1,0:T(1,128)S(1)} %reshape.29), channel_id=1, replica_groups=mesh['img'=8,'atom'=4] {'atom'}, dimensions={0} | all-to-all | bytes 786432 | tf_op jit(solution)/shard_map/all_to_all | solution.py:154
  202.7 0.5 broadcast.31
  203.2 1.8 reduce
  204.9 8.7 %reshape.30 = f32[4096,3,8]{2,1,0:T(4,128)} reshape(f32[4,24576]{1,0:T(4,128)S(1)} %reduce) | data formatting | bytes 786432
  213.6 7.4 %copy.15 = f32[3,4,8,1024]{3,2,1,0:T(8,128)} copy(f32[3,4,8,1024]{2,0,3,1:T(4,128)} %bitcast.14) | data formatting | bytes 786432 | tf_op jit(solution)/shard_map/all_to_all | solution.py:154
  (2 shorter events, 0.0 us)
Async XLA Ops:
  2.1 19.4 %all-to-all-start = ((f32[3,32,1024]{2,0,1:T(4,128)}), f32[3,32,1024]{2,0,1:T(4,128)S(1)}, u32[]{:S(2)}, u32[]{:S(2)}) async-start(f32[3,32,1024]{2,0,1:T(4,128)} %copy.11), calls=%async_computation | async-start | bytes 1048576 | tf_op jit(solution)/shard_map/all_to_all | solution.py:127
  21.7 0.7 copy-start
  125.4 9.9 %collective-permute-start = (f32[3,1,4096]{2,1,0:T(1,128)S(1)}, f32[3,1,4096]{2,1,0:T(1,128)S(1)}, u32[]{:S(2)}, u32[]{:S(2)}) collective-permute-start(f32[3,1,4096]{2,1,0:T(1,128)S(1)} %get-tuple-element.11), channel_id=1, source_target_pairs={{0,1},{1,2},{2,3},{3,4},{4,5},{5,6},{6,7},{7,8},{8,9},{9,10},{10,1... | collective-permute-start | bytes 147464 | tf_op jit(solution)/shard_map/ppermute | solution.py:132
  128.0 46.8 %collective-permute-start.1 = (f32[3,1,4096]{2,1,0:T(1,128)S(1)}, f32[3,1,4096]{2,1,0:T(1,128)S(1)}, u32[]{:S(2)}, u32[]{:S(2)}) collective-permute-start(f32[3,1,4096]{2,1,0:T(1,128)S(1)} %get-tuple-element.12), channel_id=1, source_target_pairs={{1,0},{2,1},{3,2},{4,3},{5,4},{6,5},{7,6},{8,7},{9,8},{10,9},{11,1... | collective-permute-start | bytes 147464 | tf_op jit(solution)/shard_map/ppermute | solution.py:133
